TPU v7x, 32 devices: a whole 2x2x4 slice. The times are simulated.
32 devices in a mesh: bank: 4 (over y, x), zero: 8 (over z, core).
Axes of the slice: x: 2, y: 2, z: 4, core: 2. Of those that a mesh axis runs over, the one named last changes fastest.
Arguments:
- train_gate: float32 [64, 2048, 1024], P('bank', 'zero'), may hold values from -0.1875 to 0.1875
- train_up: float32 [64, 2048, 1024], P('bank', 'zero'), may hold values from -0.1875 to 0.1875
- train_down: float32 [64, 1024, 2048], P('bank', None, 'zero'), may hold values from -0.25 to 0.25
- router_weight: float32 [2048, 64], P('zero', 'bank'), may hold values from -0.125 to 0.125
- router_gain: float32 [2048], P('zero'), may hold values from 0.25 to 1.75
Outputs:
- ready_gate: bfloat16 [64, 2048, 1024], P('bank', None, 'zero')
- ready_up: bfloat16 [64, 2048, 1024], P('bank', None, 'zero')
- ready_down: bfloat16 [64, 1024, 2048], P('bank', 'zero')
- scale_gate: float32 [64, 1024], P('bank', 'zero')
- scale_up: float32 [64, 1024], P('bank', 'zero')
- scale_down: float32 [64, 1024], P('bank', 'zero')
- serve_router: bfloat16 [2048, 64], replicated
All inputs are finite; a program needn't handle non-finite values.
Results may differ from a plain program's by a relative error of at most 0.001.
Values may be sent and summed in bfloat16 or wider, within the bound.
A program may use at most 192 MiB of HBM per device.

v0:
```python
import jax
import jax.numpy as jnp
from jax import lax
from jax.sharding import PartitionSpec as P


def on_device(train_gate, train_up, train_down, router_weight, router_gain):
    total_gate, total_up, total_down = lax.psum(
        (
            jnp.sum(train_gate * train_gate, axis=1),
            jnp.sum(train_up * train_up, axis=1),
            jnp.sum(train_down * train_down, axis=2),
        ),
        "zero",
    )
    scale_gate = jnp.sqrt(total_gate)
    scale_up = jnp.sqrt(total_up)
    scale_down = jnp.sqrt(total_down)
    narrow_gate, narrow_up, narrow_down = (
        (train_gate / jnp.expand_dims(scale_gate, 1)).astype(jnp.bfloat16),
        (train_up / jnp.expand_dims(scale_up, 1)).astype(jnp.bfloat16),
        (train_down / jnp.expand_dims(scale_down, 2)).astype(jnp.bfloat16),
    )
    ready_gate, ready_up = (
        lax.all_to_all(narrow_gate, "zero", split_axis=2, concat_axis=1, tiled=True),
        lax.all_to_all(narrow_up, "zero", split_axis=2, concat_axis=1, tiled=True),
    )
    ready_down = lax.all_to_all(narrow_down, "zero", split_axis=1, concat_axis=2, tiled=True)
    scale_gate = lax.dynamic_slice_in_dim(
        scale_gate, lax.axis_index("zero") * ready_gate.shape[2], ready_gate.shape[2], axis=1
    )
    scale_up = lax.dynamic_slice_in_dim(
        scale_up, lax.axis_index("zero") * ready_up.shape[2], ready_up.shape[2], axis=1
    )
    scale_down = lax.dynamic_slice_in_dim(
        scale_down, lax.axis_index("zero") * ready_down.shape[1], ready_down.shape[1], axis=1
    )
    part_router = (router_weight * router_gain[:, None]).astype(jnp.bfloat16)
    row_router = lax.all_gather(part_router, "zero", axis=0, tiled=True)
    serve_router = lax.all_gather(row_router, "bank", axis=1, tiled=True)
    return (ready_gate, ready_up, ready_down, scale_gate, scale_up, scale_down, serve_router)


def solution(mesh):
    return jax.shard_map(
        on_device,
        mesh=mesh,
        in_specs=(
            P("bank", "zero", None),
            P("bank", "zero", None),
            P("bank", None, "zero"),
            P("zero", "bank"),
            P("zero"),
        ),
        out_specs=(
            P("bank", None, "zero"),
            P("bank", None, "zero"),
            P("bank", "zero", None),
            P("bank", "zero"),
            P("bank", "zero"),
            P("bank", "zero"),
            P(),
        ),
        check_vma=False,
    )
```

profile of v0, /device:TPU:0, one launch (start us, length us, event | category | flops | bytes accessed | tf_op | source)
XLA Modules:
  0.0 737.9 jit_solution(13230997140834230480)
XLA Ops:
  7.2 0.0 all-reduce.3.cloned.1.call-start
  7.2 8.6 %multiply_reduce_fusion = f32[16,1024]{1,0:T(8,128)} fusion(f32[16,1024,256]{2,1,0:T(8,128)} %param.7), kind=kLoop, calls=%fused_computation.2 | loop fusion | flops 8372224 | bytes 16842752 | tf_op jit(solution)/shard_map/reduce_sum | solution.py:12
  15.8 12.6 %multiply_reduce_fusion.1 = (f32[16,1024]{1,0:T(8,128)}, f32[16,1024]{1,0:T(8,128)}) fusion(f32[16,256,1024]{2,1,0:T(8,128)} %param.6, f32[16,256,1024]{2,1,0:T(8,128)} %param.5), kind=kLoop, calls=%fused_computation.4 | loop fusion | flops 16744448 | bytes 33685504 | tf_op jit(solution)/shard_map/reduce_sum | solution.py:11
  28.4 0.0 all-reduce.3.cloned.1.call-update
  28.4 17.6 %copy.19 = f32[16,256,1024]{1,0,2:T(8,128)} copy(f32[16,256,1024]{2,1,0:T(8,128)} %param.6) | data formatting | bytes 33554432 | tf_op args[1]
  46.0 40.8 %all-reduce.3.cloned.1.call-done = (f32[16,1024]{1,0:T(8,128)}, f32[16,1024]{1,0:T(8,128)}, f32[16,1024]{1,0:T(8,128)}) async-done(((f32[16,1024]{1,0:T(8,128)}, f32[16,1024]{1,0:T(8,128)}, f32[16,1024]{1,0:T(8,128)}), (f32[16,1024]{1,0:T(8,128)}, f32[16,1024]{1,0:T(8,128)}, f32[16,1024]{1,0:T(8,128)})) %all-reduce.3.cloned.1.call-update) | async-done | bytes 196624 | tf_op jit(solution)/shard_map/psum | solution.py:8
  86.8 0.9 sqrt.10
  87.7 0.2 copy.18
  87.9 9.6 %divide_convert_fusion = bf16[16,256,1024]{1,0,2:T(8,128)(2,1)} fusion(f32[16,256,1024]{1,0,2:T(8,128)} %copy.19, f32[16,1024]{0,1:T(8,128)S(1)} %copy.18), kind=kLoop, calls=%fused_computation.3 | loop fusion | flops 8388608 | bytes 25231360 | tf_op jit(solution)/shard_map/convert_element_type | solution.py:21
  97.5 4.9 all-to-all-start.1
  102.5 0.0 copy-start.1
  102.5 17.6 %copy.16 = f32[16,256,1024]{1,0,2:T(8,128)} copy(f32[16,256,1024]{2,1,0:T(8,128)} %param.5) | data formatting | bytes 33554432 | tf_op args[0]
  120.1 0.0 copy-done.1
  120.1 0.2 copy.15
  120.3 0.0 copy-start
  120.3 9.7 %divide_convert_fusion.1 = bf16[16,256,1024]{1,0,2:T(8,128)(2,1)} fusion(f32[16,256,1024]{1,0,2:T(8,128)} %copy.16, f32[16,1024]{0,1:T(8,128)S(1)} %copy.15), kind=kLoop, calls=%fused_computation.5 | loop fusion | flops 8388608 | bytes 25231360 | tf_op jit(solution)/shard_map/convert_element_type | solution.py:20
  130.0 156.3 %all-to-all-done.1 = bf16[16,256,1024]{1,0,2:T(8,128)(2,1)} async-done(((bf16[16,256,1024]{1,0,2:T(8,128)(2,1)}), bf16[16,256,1024]{1,0,2:T(8,128)(2,1)}, u32[]{:S(2)}, u32[]{:S(2)}) %all-to-all-start.1) | async-done | bytes 8388640 | tf_op jit(solution)/shard_map/all_to_all | solution.py:26
  286.3 4.9 all-to-all-start
  291.3 0.0 copy-done
  291.3 0.2 copy.21
  291.5 0.0 copy-start.2
  291.5 0.0 copy-start.3
  291.5 16.6 %fusion = bf16[16,1024,256]{2,0,1:T(8,128)(2,1)} fusion(f32[16,1024,256]{2,1,0:T(8,128)} %param.7, f32[16,1024]{0,1:T(8,128)S(1)} %copy.21), kind=kLoop, calls=%fused_computation.1 | loop fusion | flops 8388608 | bytes 25231360 | tf_op jit(solution)/shard_map/convert_element_type | solution.py:22
  308.2 167.0 %all-to-all-done = bf16[16,256,1024]{1,0,2:T(8,128)(2,1)} async-done(((bf16[16,256,1024]{1,0,2:T(8,128)(2,1)}), bf16[16,256,1024]{1,0,2:T(8,128)(2,1)}, u32[]{:S(2)}, u32[]{:S(2)}) %all-to-all-start) | async-done | bytes 8388640 | tf_op jit(solution)/shard_map/all_to_all | solution.py:25
  475.1 5.0 all-to-all-start.2
  480.2 0.0 copy-done.2
  480.2 0.0 copy-done.3
  480.2 189.9 %all_gather.6 = bf16[2048,16]{0,1:T(8,128)(2,1)S(1)} all-gather(bf16[256,16]{0,1:T(8,128)(2,1)S(1)} %multiply_convert_fusion), channel_id=1, replica_groups=mesh['bank'=4,'zero'=8] {'zero'}, dimensions={0}, use_global_device_ids=true | all-gather | bytes 73728 | tf_op jit(solution)/shard_map/all_gather | solution.py:39
  670.1 9.1 %all_gather.7 = bf16[2048,64]{0,1:T(8,128)(2,1)S(1)} all-gather(bf16[2048,16]{0,1:T(8,128)(2,1)S(1)} %all_gather.6), channel_id=1, replica_groups=mesh['bank'=4,'zero'=8] {'bank'}, dimensions={1}, use_global_device_ids=true | all-gather | bytes 327680 | tf_op jit(solution)/shard_map/all_gather | solution.py:40
  679.2 0.6 constant_dynamic-slice_fusion
  679.8 0.6 constant_dynamic-slice_fusion.1
  680.4 0.6 constant_dynamic-slice_fusion.2
  681.0 12.3 %copy.20 = bf16[16,8,256,128]{3,2,1,0:T(8,128)(2,1)} copy(bf16[16,8,256,128]{2,0,3,1:T(8,128)(2,1)} %bitcast.4) | data formatting | bytes 16777216 | tf_op jit(solution)/shard_map/all_to_all | solution.py:26
  693.3 12.3 %copy.17 = bf16[16,8,256,128]{3,2,1,0:T(8,128)(2,1)} copy(bf16[16,8,256,128]{2,0,3,1:T(8,128)(2,1)} %bitcast.1) | data formatting | bytes 16777216 | tf_op jit(solution)/shard_map/all_to_all | solution.py:25
  705.6 0.0 all-to-all-done.2
  705.6 11.4 %copy.23 = bf16[16,128,8,256]{3,2,1,0:T(8,128)(2,1)} copy(bf16[16,128,8,256]{3,0,1,2:T(8,128)(2,1)} %bitcast.7) | data formatting | bytes 16777216 | tf_op jit(solution)/shard_map/all_to_all | solution.py:28
  716.9 13.4 %all_to_all.50 = bf16[16,128,2048]{2,1,0:T(8,128)(2,1)} reshape(bf16[16,128,8,256]{3,2,1,0:T(8,128)(2,1)} %copy.23) | data formatting | bytes 16777216 | tf_op jit(solution)/shard_map/all_to_all | solution.py:28
  730.3 0.7 copy.31
  (3 shorter events, 0.0 us)
Async XLA Ops:
  7.2 79.6 %all-reduce.3.cloned.1.call-start = ((), (), s32[]{:S(2)}) async-start(), calls=%async_computation.3 | async-start | bytes 393216 | tf_op jit(solution)/shard_map/psum | solution.py:8
  97.5 188.8 %all-to-all-start.1 = ((bf16[16,256,1024]{1,0,2:T(8,128)(2,1)}), bf16[16,256,1024]{1,0,2:T(8,128)(2,1)}, u32[]{:S(2)}, u32[]{:S(2)}) async-start(bf16[16,256,1024]{1,0,2:T(8,128)(2,1)} %divide_convert_fusion), calls=%async_computation.1 | async-start | bytes 16777216 | tf_op jit(solution)/shard_map/all_to_all | solution.py:26
  102.5 17.6 %copy-start.1 = (f32[16,1024]{1,0:T(8,128)S(1)}, f32[16,1024]{1,0:T(8,128)}, u32[]{:S(2)}) copy-start(f32[16,1024]{1,0:T(8,128)} %get-tuple-element.7) | copy-start | bytes 196612
  120.3 171.0 %copy-start = (f32[16,1024]{1,0:T(8,128)S(1)}, f32[16,1024]{1,0:T(8,128)}, u32[]{:S(2)}) copy-start(f32[16,1024]{1,0:T(8,128)} %get-tuple-element.9) | copy-start | bytes 196612
  286.3 188.8 %all-to-all-start = ((bf16[16,256,1024]{1,0,2:T(8,128)(2,1)}), bf16[16,256,1024]{1,0,2:T(8,128)(2,1)}, u32[]{:S(2)}, u32[]{:S(2)}) async-start(bf16[16,256,1024]{1,0,2:T(8,128)(2,1)} %divide_convert_fusion.1), calls=%async_computation | async-start | bytes 16777216 | tf_op jit(solution)/shard_map/all_to_all | solution.py:25
  291.5 188.7 %copy-start.2 = (f32[256,16]{0,1:T(8,128)S(1)}, f32[256,16]{0,1:T(8,128)}, u32[]{:S(2)}) copy-start(f32[256,16]{0,1:T(8,128)} %param.8) | copy-start | bytes 49156
  291.5 188.7 %copy-start.3 = (f32[256]{0:T(256)S(1)}, f32[256]{0:T(256)}, u32[]{:S(2)}) copy-start(f32[256]{0:T(256)} %param.9) | copy-start | bytes 3076
  475.1 230.4 %all-to-all-start.2 = ((bf16[16,1024,256]{2,0,1:T(8,128)(2,1)}), bf16[16,1024,256]{2,0,1:T(8,128)(2,1)}, u32[]{:S(2)}, u32[]{:S(2)}) async-start(bf16[16,1024,256]{2,0,1:T(8,128)(2,1)} %fusion), calls=%async_computation.2 | async-start | bytes 16777216 | tf_op jit(solution)/shard_map/all_to_all | solution.py:28
Sparse Core Ops, SparseCore 0:
  28.6 58.1 all-reduce.2
where the time goes:
time: 740 us; the launch traced here: 738 us
  waiting for transfers between devices  364 us (49%)
  blocking collectives  199 us (27%)
  local copies, waits for them, and re-layouts  88.6 us (12%)
  other arithmetic  57.2 us (8%)
  starting transfers between devices  14.9 us (2%)
  between operations  14.2 us (2%)
    all_gather x1, blocking collectives, on_device(): row_router = lax.all_gather(part_router, 'zero', axis=0, tiled=True)  190 us
    all_to_all x1, waiting for transfers between devices, on_device(): lax.all_to_all(narrow_gate, 'zero', split_axis=2, concat_axis=1, tiled=True)  167 us
    all_to_all x1, waiting for transfers between devices, on_device(): lax.all_to_all(narrow_up, 'zero', split_axis=2, concat_axis=1, tiled=True)  156 us
    psum x1, waiting for transfers between devices, on_device(): lax.psum((jnp.sum(train_gate * train_gate, axis=1), jnp.sum(train_up * tr...  40.8 us
    unnamed x11, local copies, waits for them, and re-layouts  35.9 us
    all_to_all x2, local copies, waits for them, and re-layouts, on_device(): lax.all_to_all(narrow_down, 'zero', split_axis=1, concat_axis=2, tiled=True)  24.8 us
    convert_element_type x1, other arithmetic, on_device(): (train_down / jnp.expand_dims(scale_down, 2)).astype(jnp.bfloat16)  16.6 us
  transfers between devices with their start and end apart: 4, of which 3 were waited for; matrix products, arithmetic and copies ran while one was open for 12% of the time, Pallas kernels for 0%

commit v1 on v0

--- a/solution.py
+++ b/solution.py
@@ -1,10 +1,134 @@
+import functools
+
 import jax
 import jax.numpy as jnp
 from jax import lax
+from jax.experimental import pallas as pl
+from jax.experimental.pallas import tpu as pltpu
 from jax.sharding import PartitionSpec as P
 
-
-def on_device(train_gate, train_up, train_down, router_weight, router_gain):
+MESH = pl.DeviceIdType.MESH
+
+
+def exchange(
+    n, chunk, near,
+    gate, up, down, scale_gate, scale_up, scale_down,
+    out_gate, out_up, out_down,
+    wide, tall, send_gate, send_up, send_down, load_sem, send_sem, recv_sem,
+):
+    me = lax.axis_index("zero")
+    experts = gate.shape[0]
+    outs = (out_gate, out_up, out_down)
+    sends = (send_gate, send_up, send_down)
+
+    def place(t, first, count):
+        if t < 2:
+            rows = gate.shape[1]
+            return outs[t].at[pl.ds(first, count), pl.ds(me * rows, rows), :]
+        cols = down.shape[2]
+        return outs[t].at[pl.ds(first, count), :, pl.ds(pl.multiple_of(me * cols, cols), cols)]
+
+    def send(t, to, first, count):
+        pltpu.make_async_remote_copy(
+            src_ref=sends[t].at[to, pl.ds(first, count)],
+            dst_ref=place(t, first, count),
+            send_sem=send_sem.at[t],
+            recv_sem=recv_sem.at[t],
+            device_id={"zero": to},
+            device_id_type=MESH,
+        ).start()
+
+    def send_at(t, distance, first, count):
+        @pl.when(me + distance < n)
+        def _():
+            send(t, me + distance, first, count)
+
+        @pl.when(me - distance >= 0)
+        def _():
+            send(t, me - distance, first, count)
+
+    for t, (source, scale, buffer) in enumerate(
+        ((gate, scale_gate, wide), (up, scale_up, wide), (down, scale_down, tall))
+    ):
+
+        def load(e):
+            slot = lax.rem(e, 2)
+            return pltpu.make_async_copy(source.at[e], buffer.at[slot], load_sem.at[slot])
+
+        load(0).start()
+
+        def narrow(e):
+            @pl.when(e + 1 < experts)
+            def _():
+                load(e + 1).start()
+
+            load(e).wait()
+            slot = lax.rem(e, 2)
+            if t < 2:
+                width = source.shape[2] // n
+                for d in range(n):
+                    part = slice(d * width, (d + 1) * width)
+                    inverse = 1.0 / scale[e, :, part]
+                    sends[t][d, e] = (buffer[slot, :, part] * inverse).astype(jnp.bfloat16)
+            else:
+                height = source.shape[1] // n
+                for d in range(n):
+                    part = slice(d * height, (d + 1) * height)
+                    inverse = 1.0 / scale[e, :, part]
+                    column = jnp.transpose(jnp.broadcast_to(inverse, (128, height)))[:, :1]
+                    sends[t][d, e] = (buffer[slot, part, :] * column).astype(jnp.bfloat16)
+
+        def group(g, _):
+            first = g * chunk
+            lax.fori_loop(0, chunk, lambda k, _: narrow(first + k), None)
+            for distance in range(1, near + 1):
+                send_at(t, distance, first, chunk)
+
+        lax.fori_loop(0, experts // chunk, group, None)
+        pltpu.make_async_copy(sends[t].at[me], place(t, 0, experts), recv_sem.at[t]).start()
+
+    for distance in range(near + 1, n):
+        for t in range(3):
+            send_at(t, distance, 0, experts)
+
+    for t in range(3):
+        others = sends[t].at[pl.ds(0, n - 1)]
+        pltpu.make_async_copy(others, others, send_sem.at[t]).wait()
+        pltpu.make_async_copy(outs[t], outs[t], recv_sem.at[t]).wait()
+
+
+def exchange_call(n, gate, up, down, scale_gate, scale_up, scale_down):
+    experts, rows, columns = gate.shape
+    _, tall, short = down.shape
+    hbm = pl.BlockSpec(memory_space=pl.ANY)
+    vmem = pl.BlockSpec(memory_space=pltpu.VMEM)
+    chunk = 2 if experts % 2 == 0 else 1
+    return pl.pallas_call(
+        functools.partial(exchange, n, chunk, min(3, n - 1)),
+        out_shape=(
+            jax.ShapeDtypeStruct((experts, rows * n, columns // n), jnp.bfloat16),
+            jax.ShapeDtypeStruct((experts, rows * n, columns // n), jnp.bfloat16),
+            jax.ShapeDtypeStruct((experts, tall // n, short * n), jnp.bfloat16),
+        ),
+        in_specs=[hbm] * 3 + [vmem] * 3,
+        out_specs=(hbm, hbm, hbm),
+        scratch_shapes=[
+            pltpu.VMEM((2, rows, columns), jnp.float32),
+            pltpu.VMEM((2, tall, short), jnp.float32),
+            pltpu.VMEM((n, experts, rows, columns // n), jnp.bfloat16),
+            pltpu.VMEM((n, experts, rows, columns // n), jnp.bfloat16),
+            pltpu.VMEM((n, experts, tall // n, short), jnp.bfloat16),
+            pltpu.SemaphoreType.DMA((2,)),
+            pltpu.SemaphoreType.DMA((3,)),
+            pltpu.SemaphoreType.DMA((3,)),
+        ],
+        compiler_params=pltpu.CompilerParams(
+            has_side_effects=True, vmem_limit_bytes=48 * 1024 * 1024
+        ),
+    )(gate, up, down, scale_gate, scale_up, scale_down)
+
+
+def on_device(n, train_gate, train_up, train_down, router_weight, router_gain):
     total_gate, total_up, total_down = lax.psum(
         (
             jnp.sum(train_gate * train_gate, axis=1),
@@ -16,16 +140,31 @@
     scale_gate = jnp.sqrt(total_gate)
     scale_up = jnp.sqrt(total_up)
     scale_down = jnp.sqrt(total_down)
-    narrow_gate, narrow_up, narrow_down = (
-        (train_gate / jnp.expand_dims(scale_gate, 1)).astype(jnp.bfloat16),
-        (train_up / jnp.expand_dims(scale_up, 1)).astype(jnp.bfloat16),
-        (train_down / jnp.expand_dims(scale_down, 2)).astype(jnp.bfloat16),
-    )
-    ready_gate, ready_up = (
-        lax.all_to_all(narrow_gate, "zero", split_axis=2, concat_axis=1, tiled=True),
-        lax.all_to_all(narrow_up, "zero", split_axis=2, concat_axis=1, tiled=True),
-    )
-    ready_down = lax.all_to_all(narrow_down, "zero", split_axis=1, concat_axis=2, tiled=True)
+    aligned = (
+        train_gate.shape[2] % (128 * n) == 0
+        and train_down.shape[1] % (128 * n) == 0
+        and train_down.shape[2] % 128 == 0
+        and train_gate.shape[1] % 16 == 0
+    )
+    if aligned:
+        ready_gate, ready_up, ready_down = exchange_call(
+            n,
+            train_gate,
+            train_up,
+            train_down,
+            *(s[:, None, :] for s in (scale_gate, scale_up, scale_down)),
+        )
+    else:
+        narrow_gate, narrow_up, narrow_down = (
+            (train_gate / jnp.expand_dims(scale_gate, 1)).astype(jnp.bfloat16),
+            (train_up / jnp.expand_dims(scale_up, 1)).astype(jnp.bfloat16),
+            (train_down / jnp.expand_dims(scale_down, 2)).astype(jnp.bfloat16),
+        )
+        ready_gate, ready_up = (
+            lax.all_to_all(narrow_gate, "zero", split_axis=2, concat_axis=1, tiled=True),
+            lax.all_to_all(narrow_up, "zero", split_axis=2, concat_axis=1, tiled=True),
+        )
+        ready_down = lax.all_to_all(narrow_down, "zero", split_axis=1, concat_axis=2, tiled=True)
     scale_gate = lax.dynamic_slice_in_dim(
         scale_gate, lax.axis_index("zero") * ready_gate.shape[2], ready_gate.shape[2], axis=1
     )
@@ -43,7 +182,7 @@
 
 def solution(mesh):
     return jax.shard_map(
-        on_device,
+        functools.partial(on_device, mesh.shape["zero"]),
         mesh=mesh,
         in_specs=(
             P("bank", "zero", None),

time: 740 us -> 672 us (0.908)
  Pallas kernels: 0 us -> 549 us
  waiting for transfers between devices: 364 us -> 33.7 us
  blocking collectives: 199 us -> 24.7 us
  local copies, waits for them, and re-layouts: 88.6 us -> 28.9 us
  other arithmetic: 57.2 us -> 21.2 us
  starting transfers between devices: 14.9 us -> 0.04 us
    pallas_call x0 -> x1, Pallas kernels: none -> 549 us  [exchange_call(): pl.pallas_call(functools.partial(exchange, n, chunk, min(3, n - 1)), out_...]
    all_to_all x3 -> x0, waiting for transfers between devices: 323 us -> none  [the longest x1 167 us: on_device(): lax.all_to_all(narrow_gate, 'zero', split_axis=2, concat_axis=1, tiled=True)]
    all_gather x1, blocking collectives: 190 us -> 15.7 us  [on_device(): row_router = lax.all_gather(part_router, 'zero', axis=0, tiled=True)]
    all_to_all x4 -> x0, local copies, waits for them, and re-layouts: 49.4 us -> none  [the longest x2 24.8 us: on_device(): lax.all_to_all(narrow_down, 'zero', split_axis=1, concat_axis=2, tiled=True)]
    convert_element_type x3 -> x0, other arithmetic: 36 us -> none  [the longest x1 16.6 us: on_device(): (train_down / jnp.expand_dims(scale_down, 2)).astype(jnp.bfloat16)]
    all_to_all x3 -> x0, starting transfers between devices: 14.9 us -> none  [the longest x1 5.01 us: on_device(): lax.all_to_all(narrow_down, 'zero', split_axis=1, concat_axis=2, tiled=True)]
    unnamed x11 -> x8, local copies, waits for them, and re-layouts: 35.9 us -> 24.3 us
  transfers between devices with their start and end apart: 4 -> 1, of which waited for: 3 -> 1; matrix products, arithmetic and copies ran while one was open for 12% -> 0% of each run, Pallas kernels for 0% -> 0%
where the time goes in v1:
time: 672 us; the launch traced here: 671 us
  Pallas kernels  549 us (82%)
  waiting for transfers between devices  33.7 us (5%)
  local copies, waits for them, and re-layouts  28.9 us (4%)
  blocking collectives  24.7 us (4%)
  other arithmetic  21.2 us (3%)
  between operations  14.1 us (2%)
    pallas_call x1, Pallas kernels, exchange_call(): pl.pallas_call(functools.partial(exchange, n, chunk, min(3, n - 1)), out_...  549 us
    psum x1, waiting for transfers between devices, on_device(): lax.psum((jnp.sum(train_gate * train_gate, axis=1), jnp.sum(train_up * tr...  33.6 us
    unnamed x8, local copies, waits for them, and re-layouts  24.3 us
    all_gather x1, blocking collectives, on_device(): row_router = lax.all_gather(part_router, 'zero', axis=0, tiled=True)  15.7 us
  transfers between devices with their start and end apart: 1, of which 1 were waited for; matrix products, arithmetic and copies ran while one was open for 0% of the time, Pallas kernels for 0%

profile of v1, /device:TPU:0, one launch (start us, length us, event | category | flops | bytes accessed | tf_op | source)
XLA Modules:
  0.0 671.1 jit_solution(8917433035571339342)
XLA Ops:
  7.2 0.0 all-reduce.3.cloned.1.call-start
  7.2 8.6 %multiply_reduce_fusion = f32[16,1024]{1,0:T(8,128)} fusion(f32[16,1024,256]{2,1,0:T(8,128)} %down.1), kind=kLoop, calls=%fused_computation | loop fusion | flops 8372224 | bytes 16842752 | tf_op jit(solution)/shard_map/reduce_sum | solution.py:136
  15.8 0.0 copy-start
  15.8 0.0 copy-start.1
  15.9 12.6 %multiply_reduce_fusion.1 = (f32[16,1024]{1,0:T(8,128)}, f32[16,1024]{1,0:T(8,128)}) fusion(f32[16,256,1024]{2,1,0:T(8,128)} %up.1, f32[16,256,1024]{2,1,0:T(8,128)} %gate.1), kind=kLoop, calls=%fused_computation.1 | loop fusion | flops 16744448 | bytes 33685504 | tf_op jit(solution)/shard_map/reduce_sum | solution.py:135
  28.4 0.0 all-reduce.3.cloned.1.call-update
  28.5 0.0 copy-done
  28.5 0.0 copy-done.1
  28.5 15.7 %all_gather.6 = bf16[2048,16]{0,1:T(8,128)(2,1)S(1)} all-gather(bf16[256,16]{0,1:T(8,128)(2,1)S(1)} %multiply_convert_fusion), channel_id=1, replica_groups=mesh['bank'=4,'zero'=8] {'zero'}, dimensions={0}, use_global_device_ids=true | all-gather | bytes 73728 | tf_op jit(solution)/shard_map/all_gather | solution.py:178
  44.2 9.1 %all_gather.7 = bf16[2048,64]{0,1:T(8,128)(2,1)S(1)} all-gather(bf16[2048,16]{0,1:T(8,128)(2,1)S(1)} %all_gather.6), channel_id=1, replica_groups=mesh['bank'=4,'zero'=8] {'bank'}, dimensions={1}, use_global_device_ids=true | all-gather | bytes 327680 | tf_op jit(solution)/shard_map/all_gather | solution.py:179
  53.2 33.6 %all-reduce.3.cloned.1.call-done = (f32[16,1024]{1,0:T(8,128)}, f32[16,1024]{1,0:T(8,128)}, f32[16,1024]{1,0:T(8,128)}) async-done(((f32[16,1024]{1,0:T(8,128)}, f32[16,1024]{1,0:T(8,128)}, f32[16,1024]{1,0:T(8,128)}), (f32[16,1024]{1,0:T(8,128)}, f32[16,1024]{1,0:T(8,128)}, f32[16,1024]{1,0:T(8,128)})) %all-reduce.3.cloned.1.call-update) | async-done | bytes 196624 | tf_op jit(solution)/shard_map/psum | solution.py:132
  86.8 0.9 sqrt.10
  87.8 0.9 sqrt.11
  88.7 0.6 constant_dynamic-slice_fusion
  89.3 0.6 constant_dynamic-slice_fusion.1
  89.9 0.9 sqrt.9
  90.8 0.6 constant_dynamic-slice_fusion.2
  91.4 548.5 %shard_map.108 = (bf16[16,2048,128]{2,1,0:T(8,128)(2,1)}, bf16[16,2048,128]{2,1,0:T(8,128)(2,1)}, bf16[16,128,2048]{2,1,0:T(8,128)(2,1)}) custom-call(f32[16,256,1024]{2,1,0:T(8,128)} %gate.1, f32[16,256,1024]{2,1,0:T(8,128)} %up.1, f32[16,1024,256]{2,1,0:T(8,128)} %down.1, f32[16,1,1024]{2,1,0:T(1,128)S(1)} %broadcast_in_dim.10.scale_gate, ...), custom_call_target="tpu_custom_call" | custom-call | tf_op jit(solution)/shard_map/pallas_call | solution.py:106
  640.0 7.6 %copy.19 = bf16[16,2048,128]{2,1,0:T(8,128)(2,1)} copy(bf16[16,2048,128]{2,1,0:T(8,128)(2,1)} %get-tuple-element.25) | data formatting | bytes 16777216
  647.5 7.6 %copy.20 = bf16[16,2048,128]{2,1,0:T(8,128)(2,1)} copy(bf16[16,2048,128]{2,1,0:T(8,128)(2,1)} %get-tuple-element.26) | data formatting | bytes 16777216
  655.1 8.4 %copy.21 = bf16[16,128,2048]{2,1,0:T(8,128)(2,1)} copy(bf16[16,128,2048]{2,1,0:T(8,128)(2,1)} %get-tuple-element.27) | data formatting | bytes 16777216
  663.6 0.7 copy.22
  (4 shorter events, 0.1 us)
Async XLA Ops:
  7.2 79.7 %all-reduce.3.cloned.1.call-start = ((), (), s32[]{:S(2)}) async-start(), calls=%async_computation | async-start | bytes 393216 | tf_op jit(solution)/shard_map/psum | solution.py:132
  15.8 12.6 %copy-start = (f32[256,16]{0,1:T(8,128)S(1)}, f32[256,16]{0,1:T(8,128)}, u32[]{:S(2)}) copy-start(f32[256,16]{0,1:T(8,128)} %param.8) | copy-start | bytes 49156
  15.8 12.6 %copy-start.1 = (f32[256]{0:T(256)S(1)}, f32[256]{0:T(256)}, u32[]{:S(2)}) copy-start(f32[256]{0:T(256)} %param.9) | copy-start | bytes 3076
Sparse Core Ops, SparseCore 0:
  28.6 58.2 all-reduce.2

commit v2 on v0

--- a/solution.py
+++ b/solution.py
@@ -1,10 +1,16 @@
+import functools
+
 import jax
 import jax.numpy as jnp
 from jax import lax
+from jax.experimental import pallas as pl
+from jax.experimental.pallas import tpu as pltpu
 from jax.sharding import PartitionSpec as P
 
-
-def on_device(train_gate, train_up, train_down, router_weight, router_gain):
+MESH = pl.DeviceIdType.MESH
+
+
+def plain(train_gate, train_up, train_down, router_weight, router_gain):
     total_gate, total_up, total_down = lax.psum(
         (
             jnp.sum(train_gate * train_gate, axis=1),
@@ -41,9 +47,275 @@
     return (ready_gate, ready_up, ready_down, scale_gate, scale_up, scale_down, serve_router)
 
 
+def exchange(
+    n, banks, chunk, near, slots,
+    gate, up, down, router, gain,
+    out_gate, out_up, out_down, scale_gate, scale_up, scale_down, out_router,
+    wide, tall, send_gate, send_up, send_down, part, got, scales, rows_router,
+    load_sem, send_sem, recv_sem, sum_send, sum_recv, scale_send, scale_recv, router_send, router_recv,
+):
+    me = lax.axis_index("zero")
+    bank = lax.axis_index("bank")
+    experts = gate.shape[0]
+    sources = (gate, up, down)
+    buffers = (wide, wide, tall)
+    outs = (out_gate, out_up, out_down)
+    sends = (send_gate, send_up, send_down)
+    width = part.shape[-1]
+
+    def to_peers(copy):
+        for distance in range(1, n):
+
+            @pl.when(me + distance < n)
+            def _():
+                copy(me + distance).start()
+
+            @pl.when(me - distance >= 0)
+            def _():
+                copy(me - distance).start()
+
+    def wait_for(refs, *sems):
+        for sem in sems:
+            pltpu.make_async_copy(refs, refs, sem).wait()
+
+    def place(t, first, count):
+        if t < 2:
+            rows = gate.shape[1]
+            return outs[t].at[pl.ds(first, count), pl.ds(me * rows, rows), :]
+        cols = down.shape[2]
+        return outs[t].at[pl.ds(first, count), :, pl.ds(pl.multiple_of(me * cols, cols), cols)]
+
+    def send(t, to, first, count):
+        pltpu.make_async_remote_copy(
+            src_ref=sends[t].at[to, pl.ds(first, count)],
+            dst_ref=place(t, first, count),
+            send_sem=send_sem.at[t],
+            recv_sem=recv_sem.at[t],
+            device_id={"zero": to},
+            device_id_type=MESH,
+        ).start()
+
+    def send_at(t, distance, first, count):
+        @pl.when(me + distance < n)
+        def _():
+            send(t, me + distance, first, count)
+
+        @pl.when(me - distance >= 0)
+        def _():
+            send(t, me - distance, first, count)
+
+    def load(t, e):
+        slot = lax.rem(e, slots)
+        return pltpu.make_async_copy(sources[t].at[e], buffers[t].at[slot], load_sem.at[slot])
+
+    def open_loads(t):
+        for e in range(min(slots - 1, experts)):
+            load(t, e).start()
+
+    def arrived(t, e):
+        @pl.when(e + slots - 1 < experts)
+        def _():
+            load(t, e + slots - 1).start()
+
+        load(t, e).wait()
+        return lax.rem(e, slots)
+
+    def sums(t):
+        open_loads(t)
+
+        def body(e, _):
+            slot = arrived(t, e)
+            for d in range(n):
+                piece = slice(d * width, (d + 1) * width)
+                if t < 2:
+                    x = buffers[t][slot, :, piece]
+                    part[t, d, e] = jnp.sum(x * x, axis=0, keepdims=True)
+                else:
+                    total = None
+                    for c in range(0, down.shape[2], 128):
+                        x = buffers[t][slot, piece, c : c + 128]
+                        total = x * x if total is None else total + x * x
+                    part[t, d, e] = jnp.sum(jnp.transpose(total), axis=0, keepdims=True)
+
+        lax.fori_loop(0, experts, body, None)
+        got[t, me] = part[t, me]
+        to_peers(
+            lambda to: pltpu.make_async_remote_copy(
+                src_ref=part.at[t, to],
+                dst_ref=got.at[t, me],
+                send_sem=sum_send.at[t],
+                recv_sem=sum_recv.at[t],
+                device_id={"zero": to},
+                device_id_type=MESH,
+            )
+        )
+
+    def finish_scale(t):
+        wait_for(got.at[t, pl.ds(0, n - 1)], sum_recv.at[t])
+        total = got[t, 0]
+        for d in range(1, n):
+            total = total + got[t, d]
+        scale = jnp.sqrt(total)
+        (scale_gate, scale_up, scale_down)[t][...] = scale
+        scales[t, me] = scale
+        to_peers(
+            lambda to: pltpu.make_async_remote_copy(
+                src_ref=scales.at[t, me],
+                dst_ref=scales.at[t, me],
+                send_sem=scale_send.at[t],
+                recv_sem=scale_recv.at[t],
+                device_id={"zero": to},
+                device_id_type=MESH,
+            )
+        )
+
+    def bulk(t):
+        open_loads(t)
+        wait_for(scales.at[t, pl.ds(0, n - 1)], scale_recv.at[t])
+
+        def narrow(e):
+            slot = arrived(t, e)
+            for d in range(n):
+                piece = slice(d * width, (d + 1) * width)
+                inverse = 1.0 / scales[t, d, e]
+                if t < 2:
+                    ready = buffers[t][slot, :, piece] * inverse
+                else:
+                    column = jnp.transpose(jnp.broadcast_to(inverse, (128, width)))[:, :1]
+                    ready = buffers[t][slot, piece, :] * column
+                sends[t][d, e] = ready.astype(jnp.bfloat16)
+
+        def group(g, _):
+            first = g * chunk
+            lax.fori_loop(0, chunk, lambda k, _: narrow(first + k), None)
+            for distance in range(1, near + 1):
+                send_at(t, distance, first, chunk)
+
+        lax.fori_loop(0, experts // chunk, group, None)
+        pltpu.make_async_copy(sends[t].at[me], place(t, 0, experts), recv_sem.at[t]).start()
+
+    height, depth = router.shape
+    block = out_router.at[pl.ds(pl.multiple_of(bank * height, height), height)]
+    spot = out_router.at[
+        pl.ds(pl.multiple_of(bank * height, height), height),
+        pl.ds(pl.multiple_of(me * depth, depth), depth),
+    ]
+    rows_router[...] = (router[...] * gain[...]).astype(jnp.bfloat16)
+
+    sums(0)
+    to_peers(
+        lambda to: pltpu.make_async_remote_copy(
+            src_ref=rows_router,
+            dst_ref=spot,
+            send_sem=router_send.at[0],
+            recv_sem=router_recv.at[0],
+            device_id={"zero": to},
+            device_id_type=MESH,
+        )
+    )
+    pltpu.make_async_copy(rows_router, spot, router_recv.at[0]).start()
+    sums(1)
+    finish_scale(0)
+    sums(2)
+    finish_scale(1)
+    wait_for(block, router_recv.at[0])
+    for step in range(1, banks):
+        pltpu.make_async_remote_copy(
+            src_ref=block,
+            dst_ref=block,
+            send_sem=router_send.at[1],
+            recv_sem=router_recv.at[1],
+            device_id={"bank": lax.rem(bank + step, banks)},
+            device_id_type=MESH,
+        ).start()
+    finish_scale(2)
+    for t in range(3):
+        bulk(t)
+    for distance in range(near + 1, n):
+        for t in range(3):
+            send_at(t, distance, 0, experts)
+
+    for t in range(3):
+        wait_for(part.at[t, pl.ds(0, n - 1)], sum_send.at[t])
+        wait_for(scales.at[t, pl.ds(0, n - 1)], scale_send.at[t])
+        wait_for(sends[t].at[pl.ds(0, n - 1)], send_sem.at[t])
+        wait_for(outs[t], recv_sem.at[t])
+    wait_for(out_router.at[pl.ds(0, height), pl.ds(0, (n - 1) * depth)], router_send.at[0])
+    wait_for(out_router.at[pl.ds(0, (banks - 1) * height)], router_send.at[1], router_recv.at[1])
+
+
+def exchange_call(n, banks, gate, up, down, router, gain):
+    experts, rows, columns = gate.shape
+    _, tall, short = down.shape
+    width = columns // n
+    height, depth = router.shape
+    hbm = pl.BlockSpec(memory_space=pl.ANY)
+    vmem = pl.BlockSpec(memory_space=pltpu.VMEM)
+    chunk = 2 if experts % 2 == 0 else 1
+    slots = min(8, experts)
+    scale = jax.ShapeDtypeStruct((experts, 1, width), jnp.float32)
+    return pl.pallas_call(
+        functools.partial(exchange, n, banks, chunk, min(3, n - 1), slots),
+        out_shape=(
+            jax.ShapeDtypeStruct((experts, rows * n, width), jnp.bfloat16),
+            jax.ShapeDtypeStruct((experts, rows * n, width), jnp.bfloat16),
+            jax.ShapeDtypeStruct((experts, width, short * n), jnp.bfloat16),
+            scale,
+            scale,
+            scale,
+            jax.ShapeDtypeStruct((height * banks, depth * n), jnp.bfloat16),
+        ),
+        in_specs=[hbm] * 3 + [vmem] * 2,
+        out_specs=(hbm, hbm, hbm, vmem, vmem, vmem, hbm),
+        scratch_shapes=[
+            pltpu.VMEM((slots, rows, columns), jnp.float32),
+            pltpu.VMEM((slots, tall, short), jnp.float32),
+            pltpu.VMEM((n, experts, rows, width), jnp.bfloat16),
+            pltpu.VMEM((n, experts, rows, width), jnp.bfloat16),
+            pltpu.VMEM((n, experts, width, short), jnp.bfloat16),
+            pltpu.VMEM((3, n, experts, 1, width), jnp.float32),
+            pltpu.VMEM((3, n, experts, 1, width), jnp.float32),
+            pltpu.VMEM((3, n, experts, 1, width), jnp.float32),
+            pltpu.VMEM((height, depth), jnp.bfloat16),
+            pltpu.SemaphoreType.DMA((slots,)),
+            pltpu.SemaphoreType.DMA((3,)),
+            pltpu.SemaphoreType.DMA((3,)),
+            pltpu.SemaphoreType.DMA((3,)),
+            pltpu.SemaphoreType.DMA((3,)),
+            pltpu.SemaphoreType.DMA((3,)),
+            pltpu.SemaphoreType.DMA((3,)),
+            pltpu.SemaphoreType.DMA((2,)),
+            pltpu.SemaphoreType.DMA((2,)),
+        ],
+        compiler_params=pltpu.CompilerParams(
+            has_side_effects=True, vmem_limit_bytes=56 * 1024 * 1024
+        ),
+    )(gate, up, down, router, gain)
+
+
+def on_device(n, banks, train_gate, train_up, train_down, router_weight, router_gain):
+    aligned = (
+        n > 1
+        and banks > 1
+        and train_gate.shape[2] == train_down.shape[1]
+        and train_gate.shape[2] == 128 * n
+        and train_down.shape[2] % 128 == 0
+        and train_gate.shape[1] % 16 == 0
+        and router_weight.shape[1] % 16 == 0
+        and router_weight.shape[0] % 128 == 0
+    )
+    if not aligned:
+        return plain(train_gate, train_up, train_down, router_weight, router_gain)
+    *ready, scale_gate, scale_up, scale_down, router = exchange_call(
+        n, banks, train_gate, train_up, train_down, router_weight.T, router_gain[None, :]
+    )
+    scales = (s[:, 0, :] for s in (scale_gate, scale_up, scale_down))
+    return (*ready, *scales, router.T)
+
+
 def solution(mesh):
     return jax.shard_map(
-        on_device,
+        functools.partial(on_device, mesh.shape["zero"], mesh.shape["bank"]),
         mesh=mesh,
         in_specs=(
             P("bank", "zero", None),

time: 740 us -> 604 us (0.82)
  Pallas kernels: 0 us -> 576 us
  waiting for transfers between devices: 364 us -> 0 us
  blocking collectives: 199 us -> 0 us
  local copies, waits for them, and re-layouts: 88.6 us -> 26.2 us
  other arithmetic: 57.2 us -> 0 us
  starting transfers between devices: 14.9 us -> 0 us
  between operations: 14.2 us -> 0.65 us
    pallas_call x0 -> x1, Pallas kernels: none -> 576 us  [exchange_call(): pl.pallas_call(functools.partial(exchange, n, banks, chunk, min(3, n - 1)...]
    all_to_all x3 -> x0, waiting for transfers between devices: 323 us -> none  [the longest x1 167 us: on_device(): lax.all_to_all(narrow_gate, 'zero', split_axis=2, concat_axis=1, tiled=True)]
    all_gather x2 -> x0, blocking collectives: 199 us -> none  [the longest x1 190 us: on_device(): row_router = lax.all_gather(part_router, 'zero', axis=0, tiled=True)]
    all_to_all x4 -> x0, local copies, waits for them, and re-layouts: 49.4 us -> none  [the longest x2 24.8 us: on_device(): lax.all_to_all(narrow_down, 'zero', split_axis=1, concat_axis=2, tiled=True)]
    psum x1 -> x0, waiting for transfers between devices: 40.8 us -> none  [on_device(): lax.psum((jnp.sum(train_gate * train_gate, axis=1), jnp.sum(train_up * tr...]
    convert_element_type x4 -> x0, other arithmetic: 36 us -> none  [the longest x1 16.6 us: on_device(): (train_down / jnp.expand_dims(scale_down, 2)).astype(jnp.bfloat16)]
    reduce_sum x2 -> x0, other arithmetic: 21.2 us -> none  [the longest x1 12.6 us: on_device(): jnp.sum(train_up * train_up, axis=1)]
    all_to_all x3 -> x0, starting transfers between devices: 14.9 us -> none  [the longest x1 5.01 us: on_device(): lax.all_to_all(narrow_down, 'zero', split_axis=1, concat_axis=2, tiled=True)]
  transfers between devices with their start and end apart: 4 -> 0, of which waited for: 3 -> 0; matrix products, arithmetic and copies ran while one was open for 12% -> 0% of each run, Pallas kernels for 0% -> 0%
where the time goes in v2:
time: 604 us; the launch traced here: 603 us
  Pallas kernels  576 us (95%)
  local copies, waits for them, and re-layouts  26.2 us (4%)
    pallas_call x1, Pallas kernels, exchange_call(): pl.pallas_call(functools.partial(exchange, n, banks, chunk, min(3, n - 1)...  576 us
    unnamed x15, local copies, waits for them, and re-layouts  26.2 us

profile of v2, /device:TPU:0, one launch (start us, length us, event | category | flops | bytes accessed | tf_op | source)
XLA Modules:
  0.0 603.3 jit_solution(18237818071814866314)
XLA Ops:
  0.6 576.5 %shard_map.108 = (bf16[16,2048,128]{2,1,0:T(8,128)(2,1)}, bf16[16,2048,128]{2,1,0:T(8,128)(2,1)}, bf16[16,128,2048]{2,1,0:T(8,128)(2,1)}, f32[16,1,128]{2,1,0:T(...) custom-call(f32[16,256,1024]{2,1,0:T(8,128)} %gate.1, f32[16,256,1024]{2,1,0:T(8,128)} %up.1, ...), custom_call_target="tpu_custom_call" | custom-call | tf_op jit(solution)/shard_map/pallas_call | solution.py:257
  577.1 7.6 %copy.19 = bf16[16,2048,128]{2,1,0:T(8,128)(2,1)} copy(bf16[16,2048,128]{2,1,0:T(8,128)(2,1)} %get-tuple-element.28) | data formatting | bytes 16777216
  584.7 7.6 %copy.20 = bf16[16,2048,128]{2,1,0:T(8,128)(2,1)} copy(bf16[16,2048,128]{2,1,0:T(8,128)(2,1)} %get-tuple-element.29) | data formatting | bytes 16777216
  592.3 0.0 copy-start.3
  592.3 0.0 copy-start.2
  592.3 0.0 copy-start.1
  592.3 0.0 copy-start
  592.3 8.5 %copy.21 = bf16[16,128,2048]{2,1,0:T(8,128)(2,1)} copy(bf16[16,128,2048]{2,1,0:T(8,128)(2,1)} %get-tuple-element.30) | data formatting | bytes 16777216
  600.8 0.0 copy-done.3
  600.8 0.6 copy.22
  601.4 0.0 copy-done.2
  601.4 0.6 copy.23
  602.0 0.0 copy-done.1
  602.0 0.6 copy.24
  602.6 0.0 copy-done
  602.6 0.7 copy.25
Async XLA Ops:
  592.3 8.5 %copy-start.3 = (f32[16,1,128]{2,1,0:T(1,128)S(1)}, f32[16,1,128]{2,1,0:T(1,128)}, u32[]{:S(2)}) copy-start(f32[16,1,128]{2,1,0:T(1,128)} %get-tuple-element.17) | copy-start | bytes 24580
  592.3 9.1 %copy-start.2 = (f32[16,1,128]{2,1,0:T(1,128)S(1)}, f32[16,1,128]{2,1,0:T(1,128)}, u32[]{:S(2)}) copy-start(f32[16,1,128]{2,1,0:T(1,128)} %get-tuple-element.18) | copy-start | bytes 24580
  592.3 9.7 %copy-start.1 = (f32[16,1,128]{2,1,0:T(1,128)S(1)}, f32[16,1,128]{2,1,0:T(1,128)}, u32[]{:S(2)}) copy-start(f32[16,1,128]{2,1,0:T(1,128)} %get-tuple-element.19) | copy-start | bytes 24580
  592.3 10.3 %copy-start = (bf16[64,2048]{1,0:T(8,128)(2,1)S(1)}, bf16[64,2048]{1,0:T(8,128)(2,1)}, u32[]{:S(2)}) copy-start(bf16[64,2048]{1,0:T(8,128)(2,1)} %get-tuple-element.20) | copy-start | bytes 786436
